TPU v7x, 128 devices: a whole 4x4x4 slice. The times are simulated.
128 devices in a mesh: scen: 32 (over x, z, core), blk: 4 (over y).
Axes of the slice: x: 4, y: 4, z: 4, core: 2. Of those that a mesh axis runs over, the one named last changes fastest.
Arguments:
- cons_matrix: bfloat16 [2048, 4096], P(None, 'blk'), may hold values from -0.09375 to 0.09375
- row_scale: float32 [2048, 2048], P('scen'), may hold values from 0.5 to 2
- rhs: float32 [2048, 2048], P('scen'), may hold values from -6 to 6
- cons_mult: float32 [2048, 2048], P('scen'), may hold values from -3 to 3
- cost: float32 [2048, 4096], P('scen', 'blk'), may hold values from -6 to 6
- ph_mult: float32 [2048, 4096], P('scen', 'blk'), may hold values from -3 to 3
- start: float32 [2048, 4096], P('scen', 'blk'), may hold values from -3 to 3
- consensus: float32 [4096], P('blk'), may hold values from -3 to 3
- upper: float32 [4096], P('blk'), may hold values from 0.3 to 1.5
- prob: float32 [2048], P('scen'), may hold values from 1 to 30, as said below
Outputs:
- solutions: float32 [2048, 4096], P('scen', 'blk')
- mult_new: float32 [2048, 2048], P('scen', 'blk')
- z_new: float32 [4096], P('blk')
- w_new: float32 [2048, 4096], P('scen', 'blk')
- primal_res: float32 [], replicated
- dual_res: float32 [], replicated
Inputs may be any that keep to these rules, and one draw needn't show every extreme that they name: prob is positive.
All inputs are finite; a program needn't handle non-finite values.
Results may differ from a plain program's by a relative error of at most 0.0017.
Values may be sent and summed in bfloat16 or wider, within the bound.
No kernel may reach another device: no remote copies, remote signals or barrier semaphores. Data moves between devices by JAX's collectives and lax.ppermute only.
A program may use at most 64 MiB of HBM per device.

v0:
```python
import jax
import jax.numpy as jnp
from jax import lax
from jax.sharding import PartitionSpec as P

NV = 4096
ITERS = 8


penalty = 1.0
aug_weight = 1.0
step_size = 0.05
eps = 1e-06


def cut_along(value, dim, peers):
    before, after = (value.shape[:dim], value.shape[dim + 1 :])
    return jnp.moveaxis(value.reshape(*before, peers, -1, *after), dim, 0)


def summed_on_arrival(value, axis, dim):
    peers = lax.axis_size(axis)
    pieces = lax.all_to_all(cut_along(value, dim, peers), axis, 0, 0, tiled=True)
    return jnp.sum(pieces.astype(jnp.float32), axis=0)


def copy_for_each(value, axis):
    copies = jnp.broadcast_to(value, (lax.axis_size(axis), *value.shape))
    return lax.all_to_all(copies, axis, split_axis=0, concat_axis=0, tiled=True)


def laid_out(pieces, dim):
    dims = list(pieces.shape[1:])
    dims[dim] *= pieces.shape[0]
    return jnp.moveaxis(pieces, 0, dim).reshape(dims)


def gathered_copies(value, axis, dim):
    pieces = copy_for_each(value, axis)
    return laid_out(pieces, dim)


def summed_on_arrival_2(value, axis, dim):
    peers = lax.axis_size(axis)
    pieces = lax.all_to_all(cut_along(value, dim, peers), axis, 0, 0, tiled=True)
    return jnp.sum(pieces, axis=0)


def of_everyone(value, axis):
    return copy_for_each(value, axis).sum(axis=0)


def together(arrays, axis):
    ends = [0]
    for a in arrays:
        ends.append(ends[-1] + a.size)
    so_far = of_everyone(jnp.concatenate([a.ravel() for a in arrays]), axis)
    return tuple((so_far[b:e].reshape(a.shape) for a, b, e in zip(arrays, ends, ends[1:])))


def per_device(
    cons_matrix, row_scale, rhs, cons_mult, cost, ph_mult, start, consensus, upper, prob
):
    n_blk = lax.axis_size("blk")
    share_rows = cons_matrix.shape[0] // n_blk
    first_row = lax.axis_index("blk") * share_rows
    own_scale = lax.dynamic_slice_in_dim(row_scale, first_row, share_rows, 1)
    own_rhs = lax.dynamic_slice_in_dim(rhs, first_row, share_rows, 1)
    own_mult = lax.dynamic_slice_in_dim(cons_mult, first_row, share_rows, 1)
    contract = (((1,), (1,)), ((), ()))
    x_now = start
    low_box = -upper[None, :]
    high_box = upper[None, :]
    for step in range(ITERS):
        partial_value = lax.dot_general(
            x_now.astype(jnp.bfloat16), cons_matrix, contract, preferred_element_type=jnp.float32
        )
        prod_share = summed_on_arrival(partial_value.astype(jnp.bfloat16), "blk", 1)
        weighted_share = (
            own_scale * (own_mult + aug_weight * (own_scale * prod_share - own_rhs))
        ).astype(jnp.bfloat16)
        back = jnp.dot(
            gathered_copies(weighted_share, "blk", 1),
            cons_matrix,
            preferred_element_type=jnp.float32,
        )
        grad = cost + ph_mult + penalty * (x_now - consensus[None, :]) + back
        x_now = jnp.clip(x_now - step_size * grad, low_box, high_box)
    partial_end = lax.dot_general(
        x_now.astype(jnp.bfloat16), cons_matrix, contract, preferred_element_type=jnp.float32
    )
    prod_end = summed_on_arrival_2(partial_end, "blk", 1)
    mult_new = own_mult + aug_weight * (own_scale * prod_end - own_rhs)
    weighted_x = prob[:, None] * x_now
    local_sum = jnp.sum(weighted_x, axis=0)
    local_total = jnp.sum(prob)
    local_square = jnp.sum(weighted_x * x_now)
    sums, total, square = together((local_sum, local_total, local_square), "scen")
    z_new = sums / total
    primal_block = square - total * jnp.sum(z_new * z_new)
    dual_block = jnp.sum((z_new - consensus) ** 2)
    primal_sum, dual_sum = lax.psum((primal_block, dual_block), "blk")
    w_new = ph_mult + penalty * (x_now - z_new[None, :])
    primal_res = jnp.sqrt(primal_sum / (total * NV) + eps)
    dual_res = penalty * jnp.sqrt(dual_sum / NV + eps)
    return (x_now, mult_new, z_new, w_new, primal_res, dual_res)


def solution(mesh):
    in_specs = (
        P(None, "blk"),
        P("scen", None),
        P("scen", None),
        P("scen", None),
        P("scen", "blk"),
        P("scen", "blk"),
        P("scen", "blk"),
        P("blk"),
        P("blk"),
        P("scen"),
    )
    out_specs = (P("scen", "blk"), P("scen", "blk"), P("blk"), P("scen", "blk"), P(), P())
    return jax.shard_map(
        per_device, mesh=mesh, in_specs=in_specs, out_specs=out_specs, check_vma=False
    )
```

profile of v0, /device:TPU:0, one launch (start us, length us, event | category | flops | bytes accessed | tf_op | source)
XLA Modules:
  0.0 231.2 jit_solution(10943974846046982356)
XLA Ops:
  0.7 3.8 %convolution_convert_fusion.7 = bf16[64,2048]{1,0:T(8,128)(2,1)S(1)} fusion(bf16[2048,1024]{1,0:T(8,128)(2,1)} %param.10, f32[64,1024]{1,0:T(8,128)} %param.16), kind=kOutput, calls=%fused_computation.7 | convolution fusion | flops 268632064 | bytes 4718592 | tf_op jit(solution)/shard_map/dot_general | solution.py:75
  5.3 4.6 %all-to-all-start = ((bf16[4,64,512]{2,1,0:T(8,128)(2,1)}), bf16[4,64,512]{2,1,0:T(8,128)(2,1)S(1)}, u32[]{:S(2)}, u32[]{:S(2)}) async-start(bf16[4,64,512]{2,1,0:T(8,128)(2,1)} %bitcast.115), calls=%async_computation | async-start | bytes 524288 | tf_op jit(solution)/shard_map/all_to_all | solution.py:23
  9.8 6.7 %all-to-all-done = bf16[4,64,512]{2,1,0:T(8,128)(2,1)S(1)} async-done(((bf16[4,64,512]{2,1,0:T(8,128)(2,1)}), bf16[4,64,512]{2,1,0:T(8,128)(2,1)S(1)}, u32[]{:S(2)}, u32[]{:S(2)}) %all-to-all-start) | async-done | bytes 262176 | tf_op jit(solution)/shard_map/all_to_all | solution.py:23
  17.4 3.4 %all-to-all-start.1 = ((bf16[4,64,512]{2,1,0:T(8,128)(2,1)}), bf16[4,64,512]{2,1,0:T(8,128)(2,1)S(1)}, u32[]{:S(2)}, u32[]{:S(2)}) async-start(bf16[4,64,512]{2,1,0:T(8,128)(2,1)} %broadcast_in_dim.18), calls=%async_computation.1 | async-start | bytes 524288 | tf_op jit(solution)/shard_map/all_to_all | solution.py:29
  20.8 6.6 %all-to-all-done.1 = bf16[4,64,512]{2,1,0:T(8,128)(2,1)S(1)} async-done(((bf16[4,64,512]{2,1,0:T(8,128)(2,1)}), bf16[4,64,512]{2,1,0:T(8,128)(2,1)S(1)}, u32[]{:S(2)}, u32[]{:S(2)}) %all-to-all-start.1) | async-done | bytes 262176 | tf_op jit(solution)/shard_map/all_to_all | solution.py:29
  27.5 3.2 %fusion.17 = f32[64,1024]{1,0:T(8,128)S(1)} fusion(f32[64,1024]{1,0:T(8,128)S(1)} %copy-done.5, bf16[64,2048]{1,0:T(8,128)(2,1)S(1)} %bitcast.124, bf16[2048,1024]{1,0:T(8,128)(2,1)} %param.10, f32[64,1024]{1,0:T(8,128)S(1)} %add.103, f32[1024]{0:T(1024)S(1)} %copy-done.8, f32[1024]{0:T(1024)S(1)} %neg.4, f32[1024]{0:T(1024)S(1)} %copy-done.7), kind=kOutput, calls=%fused_computation.33 | convolution fusion | flops 268894208 | bytes 5255168 | tf_op jit(solution)/shard_map/dot_general | solution.py:82
  32.3 9.1 %all_to_all.91 = bf16[4,64,512]{2,1,0:T(8,128)(2,1)S(1)} all-to-all(bf16[4,64,512]{2,1,0:T(8,128)(2,1)S(1)} %bitcast.135), channel_id=1, replica_groups=mesh['scen'=32,'blk'=4] {'blk'}, dimensions={0} | all-to-all | bytes 524288 | tf_op jit(solution)/shard_map/all_to_all | solution.py:23
  42.5 9.1 %all_to_all.92 = bf16[4,64,512]{2,1,0:T(8,128)(2,1)S(1)} all-to-all(bf16[4,64,512]{2,1,0:T(8,128)(2,1)S(1)} %broadcast_in_dim.19), channel_id=1, replica_groups=mesh['scen'=32,'blk'=4] {'blk'}, dimensions={0} | all-to-all | bytes 524288 | tf_op jit(solution)/shard_map/all_to_all | solution.py:29
  52.5 1.4 convolution_convert_fusion.5
  53.9 9.1 %all_to_all.93 = bf16[4,64,512]{2,1,0:T(8,128)(2,1)S(1)} all-to-all(bf16[4,64,512]{2,1,0:T(8,128)(2,1)S(1)} %bitcast.137), channel_id=1, replica_groups=mesh['scen'=32,'blk'=4] {'blk'}, dimensions={0} | all-to-all | bytes 524288 | tf_op jit(solution)/shard_map/all_to_all | solution.py:23
  64.1 9.1 %all_to_all.94 = bf16[4,64,512]{2,1,0:T(8,128)(2,1)S(1)} all-to-all(bf16[4,64,512]{2,1,0:T(8,128)(2,1)S(1)} %broadcast_in_dim.20), channel_id=1, replica_groups=mesh['scen'=32,'blk'=4] {'blk'}, dimensions={0} | all-to-all | bytes 524288 | tf_op jit(solution)/shard_map/all_to_all | solution.py:29
  74.1 1.4 convolution_convert_fusion.4
  75.6 9.7 %all_to_all.95 = bf16[4,64,512]{2,1,0:T(8,128)(2,1)S(1)} all-to-all(bf16[4,64,512]{2,1,0:T(8,128)(2,1)S(1)} %bitcast.139), channel_id=1, replica_groups=mesh['scen'=32,'blk'=4] {'blk'}, dimensions={0} | all-to-all | bytes 524288 | tf_op jit(solution)/shard_map/all_to_all | solution.py:23
  86.4 9.6 %all_to_all.96 = bf16[4,64,512]{2,1,0:T(8,128)(2,1)S(1)} all-to-all(bf16[4,64,512]{2,1,0:T(8,128)(2,1)S(1)} %broadcast_in_dim.42), channel_id=1, replica_groups=mesh['scen'=32,'blk'=4] {'blk'}, dimensions={0} | all-to-all | bytes 524288 | tf_op jit(solution)/shard_map/all_to_all | solution.py:29
  97.0 1.4 convolution_convert_fusion.3
  98.4 9.1 %all_to_all.97 = bf16[4,64,512]{2,1,0:T(8,128)(2,1)S(1)} all-to-all(bf16[4,64,512]{2,1,0:T(8,128)(2,1)S(1)} %bitcast.141), channel_id=1, replica_groups=mesh['scen'=32,'blk'=4] {'blk'}, dimensions={0} | all-to-all | bytes 524288 | tf_op jit(solution)/shard_map/all_to_all | solution.py:23
  108.6 9.1 %all_to_all.98 = bf16[4,64,512]{2,1,0:T(8,128)(2,1)S(1)} all-to-all(bf16[4,64,512]{2,1,0:T(8,128)(2,1)S(1)} %broadcast_in_dim.43), channel_id=1, replica_groups=mesh['scen'=32,'blk'=4] {'blk'}, dimensions={0} | all-to-all | bytes 524288 | tf_op jit(solution)/shard_map/all_to_all | solution.py:29
  118.6 1.4 convolution_convert_fusion.2
  120.0 9.1 %all_to_all.99 = bf16[4,64,512]{2,1,0:T(8,128)(2,1)S(1)} all-to-all(bf16[4,64,512]{2,1,0:T(8,128)(2,1)S(1)} %bitcast.143), channel_id=1, replica_groups=mesh['scen'=32,'blk'=4] {'blk'}, dimensions={0} | all-to-all | bytes 524288 | tf_op jit(solution)/shard_map/all_to_all | solution.py:23
  130.2 9.2 %all_to_all.100 = bf16[4,64,512]{2,1,0:T(8,128)(2,1)S(1)} all-to-all(bf16[4,64,512]{2,1,0:T(8,128)(2,1)S(1)} %broadcast_in_dim.44), channel_id=1, replica_groups=mesh['scen'=32,'blk'=4] {'blk'}, dimensions={0} | all-to-all | bytes 524288 | tf_op jit(solution)/shard_map/all_to_all | solution.py:29
  141.9 9.1 %all_to_all.101 = bf16[4,64,512]{2,1,0:T(8,128)(2,1)S(1)} all-to-all(bf16[4,64,512]{2,1,0:T(8,128)(2,1)S(1)} %bitcast.145), channel_id=1, replica_groups=mesh['scen'=32,'blk'=4] {'blk'}, dimensions={0} | all-to-all | bytes 524288 | tf_op jit(solution)/shard_map/all_to_all | solution.py:23
  152.1 9.1 %all_to_all.102 = bf16[4,64,512]{2,1,0:T(8,128)(2,1)S(1)} all-to-all(bf16[4,64,512]{2,1,0:T(8,128)(2,1)S(1)} %broadcast_in_dim.45), channel_id=1, replica_groups=mesh['scen'=32,'blk'=4] {'blk'}, dimensions={0} | all-to-all | bytes 524288 | tf_op jit(solution)/shard_map/all_to_all | solution.py:29
  162.1 1.4 convolution_convert_fusion
  163.5 9.1 %all_to_all.103 = bf16[4,64,512]{2,1,0:T(8,128)(2,1)S(1)} all-to-all(bf16[4,64,512]{2,1,0:T(8,128)(2,1)S(1)} %bitcast.147), channel_id=1, replica_groups=mesh['scen'=32,'blk'=4] {'blk'}, dimensions={0} | all-to-all | bytes 524288 | tf_op jit(solution)/shard_map/all_to_all | solution.py:23
  174.4 3.4 %all-to-all-start.15 = ((bf16[4,64,512]{2,1,0:T(8,128)(2,1)}), bf16[4,64,512]{2,1,0:T(8,128)(2,1)S(1)}, u32[]{:S(2)}, u32[]{:S(2)}) async-start(bf16[4,64,512]{2,1,0:T(8,128)(2,1)} %broadcast_in_dim.46), calls=%async_computation.15 | async-start | bytes 524288 | tf_op jit(solution)/shard_map/all_to_all | solution.py:29
  178.4 6.0 %all-to-all-done.15 = bf16[4,64,512]{2,1,0:T(8,128)(2,1)S(1)} async-done(((bf16[4,64,512]{2,1,0:T(8,128)(2,1)}), bf16[4,64,512]{2,1,0:T(8,128)(2,1)S(1)}, u32[]{:S(2)}, u32[]{:S(2)}) %all-to-all-start.15) | async-done | bytes 262176 | tf_op jit(solution)/shard_map/all_to_all | solution.py:29
  184.5 3.7 %fusion.32 = (f32[]{:T(128)}, f32[1024]{0:T(1024)S(1)}, f32[64,1024]{1,0:T(8,128)S(1)}) fusion(f32[64]{0:T(128)S(1)} %copy-done.11, f32[64,1024]{1,0:T(8,128)S(1)} %fusion.29, bf16[64,2048]{1,0:T(8,128)(2,1)S(1)} %bitcast.117, bf16[2048,1024]{1,0:T(8,128)(2,1)} %param.10, f32[64,1024]{1,0:T(8,128)S(1)} %add.103, f32[1024]{0:T(1024)S(1)} %copy-done.8, ...), kind=kOutput, calls=%fused_computation.59 | convolution fusion | flops 269155328 | bytes 5259524 | tf_op jit(solution)/shard_map/dot_general | solution.py:82
  190.4 8.2 %all-to-all-start.17 = ((f32[32,1,1026]{2,1,0:T(1,128)}), f32[32,1,1026]{2,1,0:T(1,128)S(1)}, u32[]{:S(2)}, u32[]{:S(2)}) async-start(f32[32,1,1026]{2,1,0:T(1,128)} %broadcast_in_dim.47), calls=%async_computation.17 | async-start | bytes 294912 | tf_op jit(solution)/shard_map/all_to_all | solution.py:29
  198.5 3.6 %fusion.33 = f32[64,2048]{1,0:T(8,128)S(1)} fusion(bf16[2048,1024]{1,0:T(8,128)(2,1)} %param.10, f32[64,1024]{1,0:T(8,128)S(1)} %get-tuple-element.15), kind=kOutput, calls=%fused_computation.70 | convolution fusion | flops 268500992 | bytes 4980736 | tf_op jit(solution)/shard_map/dot_general | solution.py:89
  202.9 3.6 %all-to-all-done.17 = f32[32,1,1026]{2,1,0:T(1,128)S(1)} async-done(((f32[32,1,1026]{2,1,0:T(1,128)}), f32[32,1,1026]{2,1,0:T(1,128)S(1)}, u32[]{:S(2)}, u32[]{:S(2)}) %all-to-all-start.17) | async-done | bytes 131360 | tf_op jit(solution)/shard_map/all_to_all | solution.py:29
  206.5 3.5 %all-to-all-start.16 = ((f32[4,64,512]{2,1,0:T(8,128)}), f32[4,64,512]{2,1,0:T(8,128)S(1)}, u32[]{:S(2)}, u32[]{:S(2)}) async-start(f32[4,64,512]{2,1,0:T(8,128)} %bitcast.99), calls=%async_computation.16 | async-start | bytes 1048576 | tf_op jit(solution)/shard_map/all_to_all | solution.py:45
  213.9 11.6 %all-reduce = (f32[]{:T(128)}, f32[]{:T(128)}) all-reduce(f32[]{:T(128)S(6)} %sub.143, f32[]{:T(128)} %get-tuple-element.8), channel_id=1, replica_groups=mesh['scen'=32,'blk'=4] {'blk'}, use_global_device_ids=true, to_apply=%region_14.15 | all-reduce | flops 2 | bytes 16 | tf_op jit(solution)/shard_map/psum | solution.py:102
  (85 shorter events, 25.9 us)
Async XLA Ops:
  0.6 26.8 %copy-start.5 = (f32[64,1024]{1,0:T(8,128)S(1)}, f32[64,1024]{1,0:T(8,128)}, u32[]{:S(2)}) copy-start(f32[64,1024]{1,0:T(8,128)} %param.16) | copy-start | bytes 786436
  0.6 15.9 %copy-start.1 = (f32[64,2048]{1,0:T(8,128)S(1)}, f32[64,2048]{1,0:T(8,128)}, u32[]{:S(2)}) copy-start(f32[64,2048]{1,0:T(8,128)} %param.12) | copy-start | bytes 1572868
  0.7 15.9 %copy-start.2 = (f32[64,2048]{1,0:T(8,128)S(1)}, f32[64,2048]{1,0:T(8,128)}, u32[]{:S(2)}) copy-start(f32[64,2048]{1,0:T(8,128)} %param.13) | copy-start | bytes 1572868
  0.7 15.9 %copy-start.3 = (f32[64,2048]{1,0:T(8,128)S(1)}, f32[64,2048]{1,0:T(8,128)}, u32[]{:S(2)}) copy-start(f32[64,2048]{1,0:T(8,128)} %param.11) | copy-start | bytes 1572868
  0.7 20.1 %copy-start.7 = (f32[1024]{0:T(1024)S(1)}, f32[1024]{0:T(1024)}, u32[]{:S(2)}) copy-start(f32[1024]{0:T(1024)} %param.18) | copy-start | bytes 12292
  0.7 20.1 %copy-start.9 = (f32[64,1024]{1,0:T(8,128)S(1)}, f32[64,1024]{1,0:T(8,128)}, u32[]{:S(2)}) copy-start(f32[64,1024]{1,0:T(8,128)} %param.14) | copy-start | bytes 786436
  0.7 20.1 %copy-start.6 = (f32[64,1024]{1,0:T(8,128)S(1)}, f32[64,1024]{1,0:T(8,128)}, u32[]{:S(2)}) copy-start(f32[64,1024]{1,0:T(8,128)} %param.15) | copy-start | bytes 786436
  0.7 26.7 %copy-start.8 = (f32[1024]{0:T(1024)S(1)}, f32[1024]{0:T(1024)}, u32[]{:S(2)}) copy-start(f32[1024]{0:T(1024)} %param.17) | copy-start | bytes 12292
  5.3 11.3 %all-to-all-start = ((bf16[4,64,512]{2,1,0:T(8,128)(2,1)}), bf16[4,64,512]{2,1,0:T(8,128)(2,1)S(1)}, u32[]{:S(2)}, u32[]{:S(2)}) async-start(bf16[4,64,512]{2,1,0:T(8,128)(2,1)} %bitcast.115), calls=%async_computation | async-start | bytes 524288 | tf_op jit(solution)/shard_map/all_to_all | solution.py:23
  17.4 10.1 %all-to-all-start.1 = ((bf16[4,64,512]{2,1,0:T(8,128)(2,1)}), bf16[4,64,512]{2,1,0:T(8,128)(2,1)S(1)}, u32[]{:S(2)}, u32[]{:S(2)}) async-start(bf16[4,64,512]{2,1,0:T(8,128)(2,1)} %broadcast_in_dim.18), calls=%async_computation.1 | async-start | bytes 524288 | tf_op jit(solution)/shard_map/all_to_all | solution.py:29
  27.4 3.4 %copy-start = (bf16[2048,1024]{1,0:T(8,128)(2,1)S(1)}, bf16[2048,1024]{1,0:T(8,128)(2,1)}, u32[]{:S(2)}) copy-start(bf16[2048,1024]{1,0:T(8,128)(2,1)} %param.10) | copy-start | bytes 12582916
  162.1 15.8 %copy-start.11 = (f32[64]{0:T(128)S(1)}, f32[64]{0:T(128)}, u32[]{:S(2)}) copy-start(f32[64]{0:T(128)} %param.19) | copy-start | bytes 772
  174.4 10.1 %all-to-all-start.15 = ((bf16[4,64,512]{2,1,0:T(8,128)(2,1)}), bf16[4,64,512]{2,1,0:T(8,128)(2,1)S(1)}, u32[]{:S(2)}, u32[]{:S(2)}) async-start(bf16[4,64,512]{2,1,0:T(8,128)(2,1)} %broadcast_in_dim.46), calls=%async_computation.15 | async-start | bytes 524288 | tf_op jit(solution)/shard_map/all_to_all | solution.py:29
  188.2 40.0 %copy-start.4 = (f32[64,1024]{1,0:T(8,128)}, f32[64,1024]{1,0:T(8,128)S(1)}, u32[]{:S(2)}) copy-start(f32[64,1024]{1,0:T(8,128)S(1)} %get-tuple-element.15) | copy-start | bytes 786436
  190.4 16.1 %all-to-all-start.17 = ((f32[32,1,1026]{2,1,0:T(1,128)}), f32[32,1,1026]{2,1,0:T(1,128)S(1)}, u32[]{:S(2)}, u32[]{:S(2)}) async-start(f32[32,1,1026]{2,1,0:T(1,128)} %broadcast_in_dim.47), calls=%async_computation.17 | async-start | bytes 294912 | tf_op jit(solution)/shard_map/all_to_all | solution.py:29
  206.5 21.7 %all-to-all-start.16 = ((f32[4,64,512]{2,1,0:T(8,128)}), f32[4,64,512]{2,1,0:T(8,128)S(1)}, u32[]{:S(2)}, u32[]{:S(2)}) async-start(f32[4,64,512]{2,1,0:T(8,128)} %bitcast.99), calls=%async_computation.16 | async-start | bytes 1048576 | tf_op jit(solution)/shard_map/all_to_all | solution.py:45
  211.9 17.1 %copy-start.10 = (f32[1024]{0:T(1024)}, f32[1024]{0:T(1024)S(1)}, u32[]{:S(2)}) copy-start(f32[1024]{0:T(1024)S(1)} %get-tuple-element.12) | copy-start | bytes 12292
where the time goes:
time: 233 us; the launch traced here: 231 us
  blocking collectives  131 us (56%)
  matrix products  29.6 us (13%)
  starting transfers between devices  23 us (10%)
  waiting for transfers between devices  22.8 us (10%)
  other arithmetic  11.3 us (5%)
  between operations  7.34 us (3%)
  local copies, waits for them, and re-layouts  6.34 us (3%)
    all_to_all x7, blocking collectives, summed_on_arrival(): lax.all_to_all(cut_along(value, dim, peers), axis, 0, 0, tiled=True)  64.1 us
    all_to_all x6, blocking collectives, copy_for_each(): return lax.all_to_all(copies, axis, split_axis=0, concat_axis=0, tiled=True)  55.1 us
    dot_general x9, matrix products, per_device(): lax.dot_general(x_now.astype(jnp.bfloat16), cons_matrix, contract, prefer...  17.1 us
    all_to_all x3, waiting for transfers between devices, copy_for_each(): return lax.all_to_all(copies, axis, split_axis=0, concat_axis=0, tiled=True)  16.1 us
    all_to_all x3, starting transfers between devices, copy_for_each(): return lax.all_to_all(copies, axis, split_axis=0, concat_axis=0, tiled=True)  15 us
    dot_general x8, matrix products, per_device(): jnp.dot(gathered_copies(weighted_share, 'blk', 1), cons_matrix, preferred...  12.5 us
    psum x1, blocking collectives, per_device(): primal_sum, dual_sum = lax.psum((primal_block, dual_block), 'blk')  11.6 us
    convert_element_type x8, other arithmetic, per_device(): weighted_share = (own_scale * (own_mult + aug_weight * (own_scale * prod_...  7.59 us
  transfers between devices with their start and end apart: 5, of which 4 were waited for; matrix products, arithmetic and copies ran while one was open for 3% of the time, Pallas kernels for 0%

commit v1 on v0

v1 whole, which is shorter than its diff:
```python
import functools

import jax
import jax.numpy as jnp
from jax import lax
from jax.experimental import pallas as pl
from jax.experimental.pallas import tpu as pltpu
from jax.sharding import Mesh
from jax.sharding import PartitionSpec as P

ITERS = 8
penalty = 1.0
aug_weight = 1.0
step_size = 0.05
eps = 1e-06

SCEN = ("x", "z", "c")
TILE = 256


def local_steps(a_hbm, state, scale, rhs, mult, x_out, m_out, a_v, at_v, x_v, w_v, sem):
    blocks, rows, width = a_hbm.shape
    own = x_v.shape[1]
    chunks = rows // TILE

    def load(b, r):
        piece = pl.ds(r * TILE, TILE)
        return pltpu.make_async_copy(a_hbm.at[b, piece], a_v.at[b, piece], sem.at[b, r])

    for b in range(blocks):
        for r in range(chunks):
            load(b, r).start()
    for b in range(blocks):
        x_v[b] = state[b, own : 2 * own]
        for r in range(chunks):
            load(b, r).wait()

        @pl.loop(0, chunks)
        def _(r):
            at = pl.ds(pl.multiple_of(r * TILE, TILE), TILE)
            for j in range(width // TILE):
                col = slice(j * TILE, (j + 1) * TILE)
                at_v[b * width + j * TILE : b * width + (j + 1) * TILE, at] = a_v[b, at, col].T

    def residual(j):
        col = slice(j * TILE, (j + 1) * TILE)
        xb = jnp.concatenate([x_v[b] for b in range(blocks)], axis=1).astype(jnp.bfloat16)
        prod = jnp.dot(xb, at_v[:, col], preferred_element_type=jnp.float32)
        return mult[:, col] + aug_weight * (scale[:, col] * prod - rhs[:, col])

    @pl.loop(0, ITERS)
    def _(i):
        for j in range(chunks):
            col = slice(j * TILE, (j + 1) * TILE)
            w_v[:, col] = (scale[:, col] * residual(j)).astype(jnp.bfloat16)
        for b in range(blocks):
            for j in range(width // TILE):
                col = slice(j * TILE, (j + 1) * TILE)
                back = jnp.dot(w_v[...], a_v[b, :, col], preferred_element_type=jnp.float32)
                x = x_v[b, :, col]
                grad = state[b, :own, col] + penalty * x + back
                box = state[b, 2 * own : 2 * own + 1, col]
                x_v[b, :, col] = jnp.clip(x - step_size * grad, -box, box)

    share = rows // blocks
    for j in range(chunks):
        at = j * TILE
        m_out[at // share, :, at % share : at % share + TILE] = residual(j)
    x_out[...] = x_v[...]


def run_local(matrix, state, scale, rhs, mult):
    blocks, rows, width = matrix.shape
    own = scale.shape[0]
    vmem = pl.BlockSpec(memory_space=pltpu.VMEM)
    return pl.pallas_call(
        local_steps,
        out_shape=(
            jax.ShapeDtypeStruct((blocks, own, width), jnp.float32),
            jax.ShapeDtypeStruct((blocks, own, rows // blocks), jnp.float32),
        ),
        in_specs=[pl.BlockSpec(memory_space=pl.ANY)] + [vmem] * 4,
        out_specs=(vmem, vmem),
        scratch_shapes=[
            pltpu.VMEM((blocks, rows, width), jnp.bfloat16),
            pltpu.VMEM((blocks * width, rows), jnp.bfloat16),
            pltpu.VMEM((blocks, own, width), jnp.float32),
            pltpu.VMEM((own, rows), jnp.bfloat16),
            pltpu.SemaphoreType.DMA((blocks, rows // TILE)),
        ],
        compiler_params=pltpu.CompilerParams(vmem_limit_bytes=48 * 1024 * 1024),
        cost_estimate=pl.CostEstimate(
            flops=2 * (2 * ITERS + 1) * own * rows * blocks * width,
            bytes_accessed=2 * blocks * rows * width,
            transcendentals=0,
        ),
        name="local_steps",
    )(matrix, state, scale, rhs, mult)


def shift(value, axis, by):
    n = lax.axis_size(axis)
    return lax.ppermute(value, axis, [(i, (i + by) % n) for i in range(n)])


def ring_sum(value, axis):
    return (value + shift(value, axis, 2)) + (shift(value, axis, 1) + shift(value, axis, 3))


def per_device(cons_matrix, row_scale, rhs, cons_mult, cost, ph_mult, start, consensus, upper, prob):
    blocks = lax.axis_size("y")
    me = lax.axis_index("y")
    rows, width = cons_matrix.shape
    group = start.shape[0]
    own = group // blocks

    n_scen = lax.axis_size(SCEN)
    piece = rows // n_scen
    mine = lax.dynamic_slice_in_dim(cons_matrix, lax.axis_index(SCEN) * piece, piece, 0)
    matrix = lax.all_gather(mine, ("y",) + SCEN).reshape(blocks, rows, width)

    linear = cost + ph_mult - penalty * consensus[None, :]
    box = jnp.broadcast_to(upper[None, None, :], (blocks, 8, width))
    sent = jnp.concatenate(
        [linear.reshape(blocks, own, width), start.reshape(blocks, own, width), box], axis=1
    )
    state = lax.all_to_all(sent, "y", 0, 0, tiled=True)
    cut = lambda a: lax.dynamic_slice_in_dim(a, me * own, own, 0)
    x_own, m_own = run_local(matrix, state, cut(row_scale), cut(rhs), cut(cons_mult))

    back = lax.all_to_all(jnp.concatenate([x_own, m_own], axis=2), "y", 0, 0, tiled=True)
    back = back.reshape(group, -1)
    x, mult_new = back[:, :width], back[:, width:]

    weighted = prob[:, None] * x
    parts = jnp.concatenate(
        [
            jnp.sum(weighted, axis=0),
            jnp.full((8,), jnp.sum(prob)),
            jnp.full((8,), jnp.sum(weighted * x)),
        ]
    )
    parts = parts + lax.ppermute(parts, "c", [(0, 1), (1, 0)])
    parts = ring_sum(ring_sum(parts, "x"), "z")
    total, square = parts[width], parts[width + 8]
    z_new = parts[:width] / total
    primal_block = square - total * jnp.sum(z_new * z_new)
    dual_block = jnp.sum((z_new - consensus) ** 2)
    norms = ring_sum(jnp.concatenate([jnp.full((8,), primal_block), jnp.full((8,), dual_block)]), "y")
    w_new = ph_mult + penalty * (x - z_new[None, :])
    n_vars = blocks * width
    primal_res = jnp.sqrt(norms[0] / (total * n_vars) + eps)
    dual_res = penalty * jnp.sqrt(norms[8] / n_vars + eps)
    return (x, mult_new, z_new, w_new, primal_res, dual_res)


def solution(mesh):
    fine = Mesh(mesh.devices.reshape(4, 4, 2, 4), SCEN + ("y",))
    in_specs = (
        P(None, "y"),
        P(SCEN, None),
        P(SCEN, None),
        P(SCEN, None),
        P(SCEN, "y"),
        P(SCEN, "y"),
        P(SCEN, "y"),
        P("y"),
        P("y"),
        P(SCEN),
    )
    out_specs = (P(SCEN, "y"), P(SCEN, "y"), P("y"), P(SCEN, "y"), P(), P())
    return jax.shard_map(
        per_device, mesh=fine, in_specs=in_specs, out_specs=out_specs, check_vma=False
    )
```

time: 233 us -> 200 us (0.86)
  blocking collectives: 131 us -> 0 us
  waiting for transfers between devices: 22.8 us -> 95.3 us
  Pallas kernels: 0 us -> 46.9 us
  matrix products: 29.6 us -> 0 us
  between operations: 7.34 us -> 20.4 us
  other arithmetic: 11.3 us -> 7.71 us
    all_to_all x13 -> x0, blocking collectives: 119 us -> none  [the longest x7 64.1 us: summed_on_arrival(): lax.all_to_all(cut_along(value, dim, peers), axis, 0, 0, tiled=True)]
    all_gather x0 -> x1, waiting for transfers between devices: none -> 66.2 us  [per_device(): matrix = lax.all_gather(mine, ('y',) + SCEN).reshape(blocks, rows, width)]
    pallas_call x0 -> x1, Pallas kernels: none -> 46.9 us  [run_local(): pl.pallas_call(local_steps, out_shape=(jax.ShapeDtypeStruct((blocks, own,...]
    dot_general x17 -> x0, matrix products: 29.6 us -> none  [the longest x9 17.1 us: per_device(): lax.dot_general(x_now.astype(jnp.bfloat16), cons_matrix, contract, prefer...]
    all_to_all x5 -> x2, starting transfers between devices: 23 us -> 8.86 us  [the longest x1 4.57 us: per_device(): state = lax.all_to_all(sent, 'y', 0, 0, tiled=True)]
    ppermute x0 -> x10, starting transfers between devices: none -> 13 us  [the longest x9 13 us: shift(): return lax.ppermute(value, axis, [(i, (i + by) % n) for i in range(n)])]
    psum x1 -> x0, blocking collectives: 11.6 us -> none  [per_device(): primal_sum, dual_sum = lax.psum((primal_block, dual_block), 'blk')]
    ppermute x0 -> x10, waiting for transfers between devices: none -> 11.2 us  [the longest x9 10.1 us: shift(): return lax.ppermute(value, axis, [(i, (i + by) % n) for i in range(n)])]
  transfers between devices with their start and end apart: 5 -> 13, of which waited for: 4 -> 9; matrix products, arithmetic and copies ran while one was open for 3% -> 3% of each run, Pallas kernels for 0% -> 0%
where the time goes in v1:
time: 200 us; the launch traced here: 199 us
  waiting for transfers between devices  95.3 us (48%)
  Pallas kernels  46.9 us (23%)
  starting transfers between devices  21.9 us (11%)
  between operations  20.4 us (10%)
  other arithmetic  7.71 us (4%)
  local copies, waits for them, and re-layouts  7.19 us (4%)
    all_gather x1, waiting for transfers between devices, per_device(): matrix = lax.all_gather(mine, ('y',) + SCEN).reshape(blocks, rows, width)  66.2 us
    pallas_call x1, Pallas kernels, run_local(): pl.pallas_call(local_steps, out_shape=(jax.ShapeDtypeStruct((blocks, own,...  46.9 us
    ppermute x9, starting transfers between devices, shift(): return lax.ppermute(value, axis, [(i, (i + by) % n) for i in range(n)])  13 us
    ppermute x9, waiting for transfers between devices, shift(): return lax.ppermute(value, axis, [(i, (i + by) % n) for i in range(n)])  10.1 us
    all_to_all x1, waiting for transfers between devices, per_device(): state = lax.all_to_all(sent, 'y', 0, 0, tiled=True)  9.87 us
    all_to_all x1, waiting for transfers between devices, per_device(): lax.all_to_all(jnp.concatenate([x_own, m_own], axis=2), 'y', 0, 0, tiled=...  7.88 us
    all_to_all x1, starting transfers between devices, per_device(): state = lax.all_to_all(sent, 'y', 0, 0, tiled=True)  4.57 us
    all_to_all x1, starting transfers between devices, per_device(): lax.all_to_all(jnp.concatenate([x_own, m_own], axis=2), 'y', 0, 0, tiled=...  4.28 us
  transfers between devices with their start and end apart: 13, of which 9 were waited for; matrix products, arithmetic and copies ran while one was open for 3% of the time, Pallas kernels for 0%

profile of v1, /device:TPU:0, one launch (start us, length us, event | category | flops | bytes accessed | tf_op | source)
XLA Modules:
  0.0 199.4 jit_solution(11663142059066692456)
XLA Ops:
  7.2 1.6 constant_dynamic-slice_fusion.3
  8.9 1.1 add_subtract_fusion
  9.9 0.7 broadcast_in_dim.8
  10.7 1.9 pad_maximum_fusion
  12.5 4.6 %all-to-all-start = ((f32[4,40,1024]{2,1,0:T(8,128)}), f32[4,40,1024]{2,1,0:T(8,128)S(1)}, u32[]{:S(2)}, u32[]{:S(2)}) async-start(f32[4,40,1024]{2,1,0:T(8,128)} %pad_maximum_fusion), calls=%async_computation | async-start | bytes 1310720 | tf_op jit(solution)/shard_map/all_to_all | solution.py:127
  17.1 1.0 constant_dynamic-slice_fusion
  18.1 9.9 %all-to-all-done.state = f32[4,40,1024]{2,1,0:T(8,128)S(1)} async-done(((f32[4,40,1024]{2,1,0:T(8,128)}), f32[4,40,1024]{2,1,0:T(8,128)S(1)}, u32[]{:S(2)}, u32[]{:S(2)}) %all-to-all-start) | async-done | bytes 655392 | tf_op jit(solution)/shard_map/all_to_all | solution.py:127
  28.0 66.2 %all-gather.3.cloned.1.call-done = bf16[8192,1024]{1,0:T(8,128)(2,1)} async-done(((bf16[64,1024]{1,0:T(8,128)(2,1)}), bf16[8192,1024]{1,0:T(8,128)(2,1)}) %all-gather.3.cloned.1.call-update) | async-done | bytes 16777232 | tf_op jit(solution)/shard_map/all_gather | solution.py:120
  94.2 46.9 %local_steps.1 = (f32[4,16,1024]{2,1,0:T(8,128)S(1)}, f32[4,16,512]{2,1,0:T(8,128)S(1)}) custom-call(bf16[4,2048,1024]{2,1,0:T(8,128)(2,1)} %bitcast.8, f32[4,40,1024]{2,1,0:T(8,128)S(1)} %all-to-all-done.state, f32[16,2048]{1,0:T(8,128)S(1)} %constant_dynamic-slice_fusion.2.scale, f32[16,2048]{1,0:T(8,128)S(1)} %get-tuple-element.21.rhs, ...), custom_call_target="tpu_custom_call" | custom-call | flops 4563402752 | bytes 16777216 | tf_op jit(solution)/shard_map/local_steps/pallas_call | solution.py:76
  141.1 0.8 pad_maximum_fusion.1
  141.9 4.3 %all-to-all-start.1 = ((f32[4,16,1536]{2,1,0:T(8,128)}), f32[4,16,1536]{2,1,0:T(8,128)S(1)}, u32[]{:S(2)}, u32[]{:S(2)}) async-start(f32[4,16,1536]{2,1,0:T(8,128)} %pad_maximum_fusion.1), calls=%async_computation.1 | async-start | bytes 786432 | tf_op jit(solution)/shard_map/all_to_all | solution.py:131
  146.8 7.9 %all-to-all-done.1 = f32[4,16,1536]{2,1,0:T(8,128)S(1)} async-done(((f32[4,16,1536]{2,1,0:T(8,128)}), f32[4,16,1536]{2,1,0:T(8,128)S(1)}, u32[]{:S(2)}, u32[]{:S(2)}) %all-to-all-start.1) | async-done | bytes 393248 | tf_op jit(solution)/shard_map/all_to_all | solution.py:131
  154.7 0.7 fusion
  155.4 0.6 broadcast_in_dim.9
  156.0 0.6 broadcast_in_dim.10
  156.8 1.2 collective-permute-done
  158.0 1.5 collective-permute-start.2
  159.4 1.8 collective-permute-start.3
  161.2 1.8 collective-permute-start.1
  163.1 3.3 %collective-permute-done.1 = f32[1040]{0:T(1024)S(1)} collective-permute-done((f32[1040]{0:T(1024)S(1)}, f32[1040]{0:T(1024)S(1)}, u32[]{:S(2)}, u32[]{:S(2)}) %collective-permute-start.1) | collective-permute-done | bytes 4192 | tf_op jit(solution)/shard_map/ppermute | solution.py:103
  166.4 1.1 collective-permute-start.5
  167.5 2.2 %collective-permute-start.6 = (f32[1040]{0:T(1024)S(1)}, f32[1040]{0:T(1024)S(1)}, u32[]{:S(2)}, u32[]{:S(2)}) collective-permute-start(f32[1040]{0:T(1024)S(1)} %add_add_fusion.1), channel_id=1, source_target_pairs={{0,24},{8,0},{16,8},{24,16},{1,25},{9,1},{17,9},{25,17},{2,26},{10... | collective-permute-start | bytes 12488 | tf_op jit(solution)/shard_map/ppermute | solution.py:103
  169.6 1.5 collective-permute-start.4
  171.1 0.7 slice.29
  171.8 3.0 %collective-permute-done.4 = f32[1040]{0:T(1024)S(1)} collective-permute-done((f32[1040]{0:T(1024)S(1)}, f32[1040]{0:T(1024)S(1)}, u32[]{:S(2)}, u32[]{:S(2)}) %collective-permute-start.4) | collective-permute-done | bytes 4192 | tf_op jit(solution)/shard_map/ppermute | solution.py:103
  175.4 1.3 multiply_reduce_fusion.1
  178.6 0.6 concatenate.15
  179.3 0.6 collective-permute-start.8
  179.9 2.7 %collective-permute-start.9 = (f32[16]{0:T(128)S(1)}, f32[16]{0:T(128)S(1)}, u32[]{:S(2)}, u32[]{:S(2)}) collective-permute-start(f32[16]{0:T(128)S(1)} %concatenate.15), channel_id=1, source_target_pairs={{0,3},{1,0},{2,1},{3,2},{4,7},{5,4},{6,5},{7,6},{8,11},{9,8},{10,9... | collective-permute-start | bytes 200 | tf_op jit(solution)/shard_map/ppermute | solution.py:103
  182.6 0.7 subtract_add_fusion
  184.1 3.5 %collective-permute-done.7 = f32[16]{0:T(128)S(1)} collective-permute-done((f32[16]{0:T(128)S(1)}, f32[16]{0:T(128)S(1)}, u32[]{:S(2)}, u32[]{:S(2)}) %collective-permute-start.7) | collective-permute-done | bytes 96 | tf_op jit(solution)/shard_map/ppermute | solution.py:103
  187.6 0.6 add_add_fusion.2
  (31 shorter events, 2.2 us)
Async XLA Ops:
  7.2 9.9 %copy-start = (f32[64,2048]{1,0:T(8,128)S(1)}, f32[64,2048]{1,0:T(8,128)}, u32[]{:S(2)}) copy-start(f32[64,2048]{1,0:T(8,128)} %param.11) | copy-start | bytes 1572868
  7.2 87.0 %all-gather.3.cloned.1.call-start = ((), (), s32[]{:S(2)}) async-start(), calls=%async_computation.2 | async-start | bytes 16908288 | tf_op jit(solution)/shard_map/all_gather | solution.py:120
  12.5 15.5 %all-to-all-start = ((f32[4,40,1024]{2,1,0:T(8,128)}), f32[4,40,1024]{2,1,0:T(8,128)S(1)}, u32[]{:S(2)}, u32[]{:S(2)}) async-start(f32[4,40,1024]{2,1,0:T(8,128)} %pad_maximum_fusion), calls=%async_computation | async-start | bytes 1310720 | tf_op jit(solution)/shard_map/all_to_all | solution.py:127
  94.2 52.0 %copy-start.5 = (f32[64]{0:T(128)S(1)}, f32[64]{0:T(128)}, u32[]{:S(2)}) copy-start(f32[64]{0:T(128)} %param.19) | copy-start | bytes 772
  94.2 81.1 %copy-start.3 = (f32[1024]{0:T(1024)S(1)}, f32[1024]{0:T(1024)}, u32[]{:S(2)}) copy-start(f32[1024]{0:T(1024)} %param.17) | copy-start | bytes 12292
  94.2 88.3 %copy-start.1 = (f32[64,1024]{1,0:T(8,128)S(1)}, f32[64,1024]{1,0:T(8,128)}, u32[]{:S(2)}) copy-start(f32[64,1024]{1,0:T(8,128)} %param.15) | copy-start | bytes 786436
  141.9 12.8 %all-to-all-start.1 = ((f32[4,16,1536]{2,1,0:T(8,128)}), f32[4,16,1536]{2,1,0:T(8,128)S(1)}, u32[]{:S(2)}, u32[]{:S(2)}) async-start(f32[4,16,1536]{2,1,0:T(8,128)} %pad_maximum_fusion.1), calls=%async_computation.1 | async-start | bytes 786432 | tf_op jit(solution)/shard_map/all_to_all | solution.py:131
  155.4 34.9 %copy-start.2 = (f32[64,1024]{1,0:T(8,128)}, f32[64,1024]{1,0:T(8,128)S(1)}, u32[]{:S(2)}) copy-start(f32[64,1024]{1,0:T(8,128)S(1)} %get-tuple-element.15) | copy-start | bytes 786436
  156.8 1.2 collective-permute-start
  158.0 5.0 %collective-permute-start.2 = (f32[1040]{0:T(1024)S(1)}, f32[1040]{0:T(1024)S(1)}, u32[]{:S(2)}, u32[]{:S(2)}) collective-permute-start(f32[1040]{0:T(1024)S(1)} %add.64), channel_id=1, source_target_pairs={{0,32},{32,64},{64,96},{96,0},{1,33},{33,65},{65,97},{97,1},{2,34}... | collective-permute-start | bytes 12488 | tf_op jit(solution)/shard_map/ppermute | solution.py:103
  159.4 3.7 %collective-permute-start.3 = (f32[1040]{0:T(1024)S(1)}, f32[1040]{0:T(1024)S(1)}, u32[]{:S(2)}, u32[]{:S(2)}) collective-permute-start(f32[1040]{0:T(1024)S(1)} %add.64), channel_id=1, source_target_pairs={{0,96},{32,0},{64,32},{96,64},{1,97},{33,1},{65,33},{97,65},{2,98}... | collective-permute-start | bytes 12488 | tf_op jit(solution)/shard_map/ppermute | solution.py:103
  161.2 5.2 %collective-permute-start.1 = (f32[1040]{0:T(1024)S(1)}, f32[1040]{0:T(1024)S(1)}, u32[]{:S(2)}, u32[]{:S(2)}) collective-permute-start(f32[1040]{0:T(1024)S(1)} %add.64), channel_id=1, source_target_pairs={{0,64},{32,96},{64,0},{96,32},{1,65},{33,97},{65,1},{97,33},{2,66}... | collective-permute-start | bytes 12488 | tf_op jit(solution)/shard_map/ppermute | solution.py:103
  166.4 5.4 %collective-permute-start.5 = (f32[1040]{0:T(1024)S(1)}, f32[1040]{0:T(1024)S(1)}, u32[]{:S(2)}, u32[]{:S(2)}) collective-permute-start(f32[1040]{0:T(1024)S(1)} %add_add_fusion.1), channel_id=1, source_target_pairs={{0,8},{8,16},{16,24},{24,0},{1,9},{9,17},{17,25},{25,1},{2,10},{10... | collective-permute-start | bytes 12488 | tf_op jit(solution)/shard_map/ppermute | solution.py:103
  167.5 4.3 %collective-permute-start.6 = (f32[1040]{0:T(1024)S(1)}, f32[1040]{0:T(1024)S(1)}, u32[]{:S(2)}, u32[]{:S(2)}) collective-permute-start(f32[1040]{0:T(1024)S(1)} %add_add_fusion.1), channel_id=1, source_target_pairs={{0,24},{8,0},{16,8},{24,16},{1,25},{9,1},{17,9},{25,17},{2,26},{10... | collective-permute-start | bytes 12488 | tf_op jit(solution)/shard_map/ppermute | solution.py:103
  169.6 5.2 %collective-permute-start.4 = (f32[1040]{0:T(1024)S(1)}, f32[1040]{0:T(1024)S(1)}, u32[]{:S(2)}, u32[]{:S(2)}) collective-permute-start(f32[1040]{0:T(1024)S(1)} %add_add_fusion.1), channel_id=1, source_target_pairs={{0,16},{8,24},{16,0},{24,8},{1,17},{9,25},{17,1},{25,9},{2,18},{10... | collective-permute-start | bytes 12488 | tf_op jit(solution)/shard_map/ppermute | solution.py:103
  176.6 13.6 %copy-start.4 = (f32[1024]{0:T(1024)}, f32[1024]{0:T(1024)S(1)}, u32[]{:S(2)}) copy-start(f32[1024]{0:T(1024)S(1)} %get-tuple-element.14) | copy-start | bytes 12292
  179.3 4.8 %collective-permute-start.8 = (f32[16]{0:T(128)S(1)}, f32[16]{0:T(128)S(1)}, u32[]{:S(2)}, u32[]{:S(2)}) collective-permute-start(f32[16]{0:T(128)S(1)} %concatenate.15), channel_id=1, source_target_pairs={{0,1},{1,2},{2,3},{3,0},{4,5},{5,6},{6,7},{7,4},{8,9},{9,10},{10,1... | collective-permute-start | bytes 200 | tf_op jit(solution)/shard_map/ppermute | solution.py:103
  179.9 4.2 %collective-permute-start.9 = (f32[16]{0:T(128)S(1)}, f32[16]{0:T(128)S(1)}, u32[]{:S(2)}, u32[]{:S(2)}) collective-permute-start(f32[16]{0:T(128)S(1)} %concatenate.15), channel_id=1, source_target_pairs={{0,3},{1,0},{2,1},{3,2},{4,7},{5,4},{6,5},{7,6},{8,11},{9,8},{10,9... | collective-permute-start | bytes 200 | tf_op jit(solution)/shard_map/ppermute | solution.py:103
  182.6 5.1 %collective-permute-start.7 = (f32[16]{0:T(128)S(1)}, f32[16]{0:T(128)S(1)}, u32[]{:S(2)}, u32[]{:S(2)}) collective-permute-start(f32[16]{0:T(128)S(1)} %concatenate.15), channel_id=1, source_target_pairs={{0,2},{1,3},{2,0},{3,1},{4,6},{5,7},{6,4},{7,5},{8,10},{9,11},{10,... | collective-permute-start | bytes 200 | tf_op jit(solution)/shard_map/ppermute | solution.py:103
Sparse Core Ops, SparseCore 0:
  11.7 82.4 all-gather.2
